TPU v7x, 32 devices: a whole 2x2x4 slice. The times are simulated.
32 devices in a mesh: col: 16 (over z, y, x), lev: 2 (over core).
Axes of the slice: x: 2, y: 2, z: 4, core: 2. Of those that a mesh axis runs over, the one named last changes fastest.
Arguments:
- perturbations: float32 [80, 16, 16384], P(None, 'lev', 'col'), may hold values from -0.625 to 0.625
- gradient: float32 [32, 16, 16384], P(None, 'lev', 'col'), may hold values from -2 to 2
- horizontal: float32 [20, 16384], P(None, 'col'), may hold values from -50 to 50
- area: float32 [16384], P('col'), may hold values from 1 to 60
- vertical: float32 [20, 16], P(None, 'lev'), may hold values from -1.25 to 1.25
Outputs:
- increment: float32 [32, 16, 16384], P(None, 'lev', 'col')
- background: float32 [32], replicated
All inputs are finite; a program needn't handle non-finite values.
Results may differ from a plain program's by a relative error of at most 0.0003.
Values sent between devices are 32-bit elements; how exact they have to be, the bound alone decides.
A program may use at most 128 MiB of HBM per device.

v0:
```python
import jax
import jax.numpy as jnp
from jax import lax
from jax.sharding import PartitionSpec as P

TOP_PRECISION = lax.Precision.HIGHEST


def adjoint_terms(perturbations, weighted, modes):
    mode_products = weighted[:, :, None, :] * modes[None, None, :, :]
    return jnp.einsum("klc,vlbc->lkvb", perturbations, mode_products, precision=TOP_PRECISION)


def project_levels(vertical, terms):
    return jnp.einsum("al,lkvb->vkab", vertical, terms, precision=TOP_PRECISION)


def mode_factor(mode_power, area_sum, count_modes):
    return 1.0 / jnp.sqrt(count_modes * (mode_power / area_sum + 1e-06))


def per_device(perturbations, gradient, horizontal, area, vertical):
    count_modes = horizontal.shape[0]
    columns = horizontal.shape[1] * lax.axis_size("col")
    power_local = jnp.sum(area[None, :] * horizontal * horizontal, axis=1)
    area_local = jnp.sum(area)
    weighted = gradient * (area * columns)[None, None, :]
    terms = adjoint_terms(perturbations, weighted, horizontal)
    summed, doubled_power, doubled = lax.psum(
        (project_levels(vertical, terms), power_local, area_local), ("col", "lev")
    )
    area_sum = doubled / lax.axis_size("lev")
    mode_power = doubled_power / lax.axis_size("lev")
    factor = mode_factor(mode_power, area_sum, count_modes)
    scaled_terms = horizontal * factor[:, None]
    control = summed * (factor / area_sum)[None, None, None, :]
    lifted = jnp.einsum("al,vkab->lkvb", vertical, control, precision=TOP_PRECISION)
    member_spread = jnp.einsum("lkvb,klc->lvbc", lifted, perturbations, precision=TOP_PRECISION)
    increment = jnp.einsum("trxa,xa->rta", member_spread, scaled_terms, precision=TOP_PRECISION)
    background = 0.5 * jnp.sum(control * control, axis=(1, 2, 3))
    return (increment, background)


def solution(mesh):
    return jax.shard_map(
        per_device,
        mesh=mesh,
        in_specs=(
            P(None, "lev", "col"),
            P(None, "lev", "col"),
            P(None, "col"),
            P("col"),
            P(None, "lev"),
        ),
        out_specs=(P(None, "lev", "col"), P()),
        check_vma=False,
    )
```

profile of v0, /device:TPU:0, one launch (start us, length us, event | category | flops | bytes accessed | tf_op | source)
XLA Modules:
  0.0 289.0 jit_solution(13503806161520612798)
XLA Ops:
  7.2 0.0 copy-start
  7.2 0.0 all-reduce.3.cloned.1.call-start
  7.2 1.4 broadcast_multiply_fusion.2
  8.7 1.3 broadcast_multiply_fusion.1
  10.0 10.6 %broadcast_multiply_fusion = f32[32,8,20,1024]{3,1,2,0:T(8,128)} fusion(f32[20,1024]{1,0:T(8,128)} %param.7, f32[32,8,1024]{2,1,0:T(8,128)S(1)} %broadcast_multiply_fusion.1), kind=kLoop, calls=%fused_computation.3 | loop fusion | flops 5242880 | bytes 22102016 | tf_op jit(solution)/shard_map/mul | solution.py:10
  20.6 0.0 copy-done
  20.6 0.0 copy-start.2
  20.6 38.6 %fusion.12 = f32[8,80,32,20]{1,2,3,0:T(8,128)S(1)} fusion(f32[80,8,1024,1]{2,1,0,3:T(8,128)S(1)} %bitcast.23, f32[32,8,20,1024]{3,1,2,0:T(8,128)} %broadcast_multiply_fusion), kind=kOutput, calls=%fused_computation.14 | convolution fusion | flops 5033164800 | bytes 25231360 | tf_op jit(solution)/shard_map/klc,vlbc->lkvb/dot_general | solution.py:11
  59.2 0.0 copy-done.2
  59.2 0.0 copy-start.1
  59.2 0.0 copy-start.3
  59.2 10.3 %convolution_bitcast_fusion = f32[32,80,20,20]{1,2,3,0:T(8,128)} fusion(f32[8,80,32,20]{1,2,3,0:T(8,128)S(1)} %fusion.12, f32[20,8]{0,1:T(8,128)S(1)} %copy-done.2), kind=kOutput, calls=%fused_computation.9 | convolution fusion | flops 98304000 | bytes 5735040 | tf_op jit(solution)/shard_map/al,lkvb->vkab/dot_general | solution.py:15
  69.5 0.0 all-reduce.3.cloned.1.call-update
  69.6 0.0 copy-done.1
  69.6 0.0 copy-done.3
  69.6 0.1 fusion.17
  69.7 43.9 %all-reduce = (f32[20]{0:T(128)S(1)}, f32[]{:T(128)}) all-reduce(f32[20]{0:T(128)S(1)} %fusion.17, f32[]{:T(128)} %get-tuple-element.7), channel_id=1, replica_groups=mesh['col'=16,'lev'=2] {'col','lev'}, use_global_device_ids=true, to_apply=%region_1.0 | all-reduce | flops 21 | bytes 168 | tf_op jit(solution)/shard_map/psum | solution.py:29
  114.3 0.1 multiply_bitcast_fusion
  114.3 132.2 %all-reduce.3.cloned.1.call-done = f32[32,80,20,20]{1,2,3,0:T(8,128)} async-done(((f32[32,80,20,20]{1,2,3,0:T(8,128)}), f32[32,80,20,20]{1,2,3,0:T(8,128)}) %all-reduce.3.cloned.1.call-update) | async-done | bytes 4096016 | tf_op jit(solution)/shard_map/psum | solution.py:29
  246.5 0.0 slice-start
  246.5 8.6 %fusion.9 = f32[8,80,32,20]{1,0,3,2:T(8,128)S(1)} fusion(f32[32,80,20,20]{1,2,3,0:T(8,128)} %all-reduce.3.cloned.1.call-done, f32[20]{0:T(128)S(1)} %get-tuple-element.4, f32[20,8]{0,1:T(8,128)S(1)} %copy-done.2), kind=kOutput, calls=%fused_computation.13 | convolution fusion | flops 99328000 | bytes 5735120 | tf_op jit(solution)/shard_map/al,vkab->lkvb/dot_general | solution.py:37
  255.2 0.0 slice-start.1
  255.2 23.4 %multiply_reduce_fusion = f32[1024,8,32]{0,2,1:T(8,128)S(1)} fusion(f32[1024,20]{0,1:T(8,128)S(1)} %multiply_bitcast_fusion, f32[8,80,32,20]{1,0,3,2:T(8,128)S(1)} %fusion.9, f32[80,8,1024,1]{2,1,0,3:T(8,128)S(1)} %bitcast.24), kind=kOutput, calls=%fused_computation | convolution fusion | flops 5043388416 | bytes 5390336 | tf_op jit(solution)/shard_map/lkvb,klc->lvbc/dot_general | solution.py:38
  278.6 1.6 copy.46
  280.2 0.0 slice-done
  280.2 0.0 slice-done.1
  280.2 1.4 multiply_reduce_fusion.1
  281.6 0.5 broadcast_multiply_fusion.3
  (2 shorter events, 0.0 us)
Async XLA Ops:
  7.2 13.4 %copy-start = (f32[80,8,1024]{2,1,0:T(8,128)S(1)}, f32[80,8,1024]{2,1,0:T(8,128)}, u32[]{:S(2)}) copy-start(f32[80,8,1024]{2,1,0:T(8,128)} %param.5) | copy-start | bytes 7864324
  7.2 239.3 %all-reduce.3.cloned.1.call-start = ((), (), s32[]{:S(2)}) async-start(), calls=%async_computation | async-start | bytes 15728640 | tf_op jit(solution)/shard_map/psum | solution.py:29
  20.6 38.6 %copy-start.2 = (f32[20,8]{0,1:T(8,128)S(1)}, f32[20,8]{0,1:T(8,128)}, u32[]{:S(2)}) copy-start(f32[20,8]{0,1:T(8,128)} %param.9) | copy-start | bytes 1924
  59.2 10.3 %copy-start.1 = (f32[20,1024]{1,0:T(8,128)S(1)}, f32[20,1024]{1,0:T(8,128)}, u32[]{:S(2)}) copy-start(f32[20,1024]{1,0:T(8,128)} %param.7) | copy-start | bytes 245764
  59.2 10.3 %copy-start.3 = (f32[1024]{0:T(1024)S(1)}, f32[1024]{0:T(1024)}, u32[]{:S(2)}) copy-start(f32[1024]{0:T(1024)} %param.8) | copy-start | bytes 12292
  246.5 33.6 %slice-start = ((s8[7864320]{0:T(1024)(128)(4,1)}), s8[4194304]{0:T(1024)(128)(4,1)S(1)}, s32[]{:S(2)}) async-start(s8[7864320]{0:T(1024)(128)(4,1)} %bitcast.25), calls=%async_computation.1 | async-start | bytes 8388608
  255.2 25.0 %slice-start.1 = ((s8[7864320]{0:T(1024)(128)(4,1)}), s8[3670016]{0:T(1024)(128)(4,1)S(1)}, s32[]{:S(2)}) async-start(s8[7864320]{0:T(1024)(128)(4,1)} %bitcast.25), calls=%async_computation.2 | async-start | bytes 7340032
Sparse Core Ops, SparseCore 0:
  69.7 176.8 all-reduce.2
where the time goes:
time: 289 us
  waiting for transfers between devices  132 us (46%)
  matrix products  80.9 us (28%)
  blocking collectives  43.9 us (15%)
  other arithmetic  15.5 us (5%)
  between operations  14.8 us (5%)
    psum x1, waiting for transfers between devices, per_device(): lax.psum((project_levels(vertical, terms), power_local, area_local), ('co...  132 us
    psum x1, blocking collectives, per_device(): lax.psum((project_levels(vertical, terms), power_local, area_local), ('co...  43.9 us
    dot_general x1, matrix products, adjoint_terms(): jnp.einsum('klc,vlbc->lkvb', perturbations, mode_products, precision=TOP_...  38.6 us
    dot_general x1, matrix products, per_device(): jnp.einsum('lkvb,klc->lvbc', lifted, perturbations, precision=TOP_PRECISION)  23.4 us
    mul x1, other arithmetic, adjoint_terms(): mode_products = weighted[:, :, None, :] * modes[None, None, :, :]  10.6 us
    dot_general x1, matrix products, project_levels(): return jnp.einsum('al,lkvb->vkab', vertical, terms, precision=TOP_PRECISION)  10.3 us
    dot_general x1, matrix products, per_device(): jnp.einsum('al,vkab->lkvb', vertical, control, precision=TOP_PRECISION)  8.63 us
  transfers between devices with their start and end apart: 1, of which 1 were waited for; matrix products, arithmetic and copies ran while one was open for 0% of the time, Pallas kernels for 0%

commit v1 on v0

--- a/solution.py
+++ b/solution.py
@@ -4,6 +4,11 @@
 from jax.sharding import PartitionSpec as P
 
 TOP_PRECISION = lax.Precision.HIGHEST
+
+
+def axis_by_axis(array, first, second):
+    partial = lax.psum(array, first)
+    return lax.psum(partial, second)
 
 
 def adjoint_terms(perturbations, weighted, modes):
@@ -26,8 +31,8 @@
     area_local = jnp.sum(area)
     weighted = gradient * (area * columns)[None, None, :]
     terms = adjoint_terms(perturbations, weighted, horizontal)
-    summed, doubled_power, doubled = lax.psum(
-        (project_levels(vertical, terms), power_local, area_local), ("col", "lev")
+    summed, doubled_power, doubled = axis_by_axis(
+        (project_levels(vertical, terms), power_local, area_local), "lev", "col"
     )
     area_sum = doubled / lax.axis_size("lev")
     mode_power = doubled_power / lax.axis_size("lev")

time: 289 us -> 402 us (1.39)
  waiting for transfers between devices: 132 us -> 241 us
    psum x1 -> x2, waiting for transfers between devices: 132 us -> 241 us  [the longest x1 203 us: axis_by_axis(): return lax.psum(partial, second)]
    psum x1 -> x2, blocking collectives: 43.9 us -> 47.6 us  [the longest x1 44.5 us: axis_by_axis(): return lax.psum(partial, second)]
  transfers between devices with their start and end apart: 1 -> 2, of which waited for: 1 -> 2; matrix products, arithmetic and copies ran while one was open for 0% -> 0% of each run, Pallas kernels for 0% -> 0%
where the time goes in v1:
time: 402 us
  waiting for transfers between devices  241 us (60%)
  matrix products  81.2 us (20%)
  blocking collectives  47.6 us (12%)
  other arithmetic  15.5 us (4%)
  between operations  14.8 us (4%)
    psum x1, waiting for transfers between devices, axis_by_axis(): return lax.psum(partial, second)  203 us
    psum x1, blocking collectives, axis_by_axis(): return lax.psum(partial, second)  44.5 us
    dot_general x1, matrix products, adjoint_terms(): jnp.einsum('klc,vlbc->lkvb', perturbations, mode_products, precision=TOP_...  38.6 us
    psum x1, waiting for transfers between devices, axis_by_axis(): partial = lax.psum(array, first)  38 us
    dot_general x1, matrix products, per_device(): jnp.einsum('lkvb,klc->lvbc', lifted, perturbations, precision=TOP_PRECISION)  23.4 us
    mul x1, other arithmetic, adjoint_terms(): mode_products = weighted[:, :, None, :] * modes[None, None, :, :]  10.6 us
    dot_general x1, matrix products, project_levels(): return jnp.einsum('al,lkvb->vkab', vertical, terms, precision=TOP_PRECISION)  10.3 us
    dot_general x1, matrix products, per_device(): jnp.einsum('al,vkab->lkvb', vertical, control, precision=TOP_PRECISION)  8.87 us
  transfers between devices with their start and end apart: 2, of which 2 were waited for; matrix products, arithmetic and copies ran while one was open for 0% of the time, Pallas kernels for 0%

profile of v1, /device:TPU:0, one launch (start us, length us, event | category | flops | bytes accessed | tf_op | source)
XLA Modules:
  0.0 402.0 jit_solution(254839177862882139)
XLA Ops:
  7.2 0.0 copy-start
  7.2 0.0 all-reduce.5.cloned.1.call-start
  7.2 1.4 broadcast_multiply_fusion.2
  8.7 1.3 broadcast_multiply_fusion.1
  10.0 10.6 %broadcast_multiply_fusion = f32[32,8,20,1024]{3,1,2,0:T(8,128)} fusion(f32[20,1024]{1,0:T(8,128)} %param.7, f32[32,8,1024]{2,1,0:T(8,128)S(1)} %broadcast_multiply_fusion.1), kind=kLoop, calls=%fused_computation.3 | loop fusion | flops 5242880 | bytes 22102016 | tf_op jit(solution)/shard_map/mul | solution.py:15
  20.6 0.0 copy-done
  20.6 0.0 copy-start.2
  20.6 38.6 %fusion.12 = f32[8,80,32,20]{1,2,3,0:T(8,128)S(1)} fusion(f32[80,8,1024,1]{2,1,0,3:T(8,128)S(1)} %bitcast.23, f32[32,8,20,1024]{3,1,2,0:T(8,128)} %broadcast_multiply_fusion), kind=kOutput, calls=%fused_computation.14 | convolution fusion | flops 5033164800 | bytes 25231360 | tf_op jit(solution)/shard_map/klc,vlbc->lkvb/dot_general | solution.py:16
  59.2 0.0 copy-done.2
  59.2 10.3 %convolution_bitcast_fusion = f32[32,80,20,20]{1,2,3,0:T(8,128)} fusion(f32[8,80,32,20]{1,2,3,0:T(8,128)S(1)} %fusion.12, f32[20,8]{0,1:T(8,128)S(1)} %copy-done.2), kind=kOutput, calls=%fused_computation.9 | convolution fusion | flops 98304000 | bytes 5735040 | tf_op jit(solution)/shard_map/al,lkvb->vkab/dot_general | solution.py:20
  69.5 0.0 copy-start.1
  69.5 0.0 copy-start.3
  69.5 0.0 all-reduce.5.cloned.1.call-update
  69.5 0.0 all-reduce.7.cloned.1.call-start
  69.6 38.0 %all-reduce.5.cloned.1.call-done = f32[32,80,20,20]{1,2,3,0:T(8,128)} async-done(((f32[32,80,20,20]{1,2,3,0:T(8,128)}), f32[32,80,20,20]{1,2,3,0:T(8,128)}) %all-reduce.5.cloned.1.call-update) | async-done | bytes 4096016 | tf_op jit(solution)/shard_map/psum | solution.py:10
  107.6 0.0 all-reduce.7.cloned.1.call-update
  107.6 0.0 copy-done.1
  107.6 0.0 copy-done.3
  107.7 0.1 fusion.17
  107.8 3.1 all-reduce.1
  110.9 44.5 %all-reduce = (f32[20]{0:T(128)S(1)}, f32[]{:T(128)}) all-reduce(f32[20]{0:T(128)S(1)} %get-tuple-element.4, f32[]{:T(128)} %get-tuple-element.5), channel_id=1, replica_groups=mesh['col'=16,'lev'=2] {'col'}, use_global_device_ids=true, to_apply=%region_2.0 | all-reduce | flops 21 | bytes 168 | tf_op jit(solution)/shard_map/psum | solution.py:11
  156.0 0.1 multiply_bitcast_fusion
  156.1 203.3 %all-reduce.7.cloned.1.call-done = f32[32,80,20,20]{1,2,3,0:T(8,128)} async-done(((f32[32,80,20,20]{1,2,3,0:T(8,128)}), f32[32,80,20,20]{1,2,3,0:T(8,128)}) %all-reduce.7.cloned.1.call-update) | async-done | bytes 4096016 | tf_op jit(solution)/shard_map/psum | solution.py:11
  359.4 0.0 slice-start
  359.4 8.9 %fusion.9 = f32[8,80,32,20]{1,0,3,2:T(8,128)S(1)} fusion(f32[32,80,20,20]{1,2,3,0:T(8,128)} %all-reduce.7.cloned.1.call-done, f32[20]{0:T(128)S(1)} %get-tuple-element.6, f32[20,8]{0,1:T(8,128)S(1)} %copy-done.2), kind=kOutput, calls=%fused_computation.13 | convolution fusion | flops 99328000 | bytes 5735120 | tf_op jit(solution)/shard_map/al,vkab->lkvb/dot_general | solution.py:42
  368.3 0.0 slice-start.1
  368.3 23.4 %multiply_reduce_fusion = f32[1024,8,32]{0,2,1:T(8,128)S(1)} fusion(f32[1024,20]{0,1:T(8,128)S(1)} %multiply_bitcast_fusion, f32[8,80,32,20]{1,0,3,2:T(8,128)S(1)} %fusion.9, f32[80,8,1024,1]{2,1,0,3:T(8,128)S(1)} %bitcast.24), kind=kOutput, calls=%fused_computation | convolution fusion | flops 5043388416 | bytes 5390336 | tf_op jit(solution)/shard_map/lkvb,klc->lvbc/dot_general | solution.py:43
  391.7 1.6 copy.46
  393.2 0.0 slice-done
  393.2 0.0 slice-done.1
  393.3 1.4 multiply_reduce_fusion.1
  394.7 0.5 broadcast_multiply_fusion.3
  (2 shorter events, 0.0 us)
Async XLA Ops:
  7.2 13.4 %copy-start = (f32[80,8,1024]{2,1,0:T(8,128)S(1)}, f32[80,8,1024]{2,1,0:T(8,128)}, u32[]{:S(2)}) copy-start(f32[80,8,1024]{2,1,0:T(8,128)} %param.5) | copy-start | bytes 7864324
  7.2 100.4 %all-reduce.5.cloned.1.call-start = ((), (), s32[]{:S(2)}) async-start(), calls=%async_computation | async-start | bytes 15728640 | tf_op jit(solution)/shard_map/psum | solution.py:10
  20.6 38.6 %copy-start.2 = (f32[20,8]{0,1:T(8,128)S(1)}, f32[20,8]{0,1:T(8,128)}, u32[]{:S(2)}) copy-start(f32[20,8]{0,1:T(8,128)} %param.9) | copy-start | bytes 1924
  69.5 38.1 %copy-start.1 = (f32[20,1024]{1,0:T(8,128)S(1)}, f32[20,1024]{1,0:T(8,128)}, u32[]{:S(2)}) copy-start(f32[20,1024]{1,0:T(8,128)} %param.7) | copy-start | bytes 245764
  69.5 38.1 %copy-start.3 = (f32[1024]{0:T(1024)S(1)}, f32[1024]{0:T(1024)}, u32[]{:S(2)}) copy-start(f32[1024]{0:T(1024)} %param.8) | copy-start | bytes 12292
  69.5 289.8 %all-reduce.7.cloned.1.call-start = ((), (), s32[]{:S(2)}) async-start(), calls=%async_computation.1 | async-start | bytes 15728640 | tf_op jit(solution)/shard_map/psum | solution.py:11
  359.4 33.9 %slice-start = ((s8[7864320]{0:T(1024)(128)(4,1)}), s8[4194304]{0:T(1024)(128)(4,1)S(1)}, s32[]{:S(2)}) async-start(s8[7864320]{0:T(1024)(128)(4,1)} %bitcast.25), calls=%async_computation.2 | async-start | bytes 8388608
  368.3 25.0 %slice-start.1 = ((s8[7864320]{0:T(1024)(128)(4,1)}), s8[3670016]{0:T(1024)(128)(4,1)S(1)}, s32[]{:S(2)}) async-start(s8[7864320]{0:T(1024)(128)(4,1)} %bitcast.25), calls=%async_computation.3 | async-start | bytes 7340032
Sparse Core Ops, SparseCore 0:
  69.7 37.9 all-reduce.4
  113.8 245.5 all-reduce.6
